TPU v7x, 32 devices: a whole 2x2x4 slice. The times are simulated.
32 devices in a mesh: gx: 4 (over z), gy: 4 (over x, core), col: 2 (over y).
Axes of the slice: x: 2, y: 2, z: 4, core: 2. Of those that a mesh axis runs over, the one named last changes fastest.
Arguments:
- fields: bfloat16 [2, 128, 128, 32, 128], P('col', 'gx', 'gy'), may hold values from -6 to 6
- spectral: bfloat16 [1, 16, 16, 2, 32, 32, 16], P(None, 'gx', 'gy', None, None, 'col'), may hold values from -0.75 to 0.75
- skip_weight: bfloat16 [1, 32, 32], replicated, may hold values from -1 to 1
- skip_bias: float32 [1, 32], replicated, may hold values from -3 to 3
- norm_gain: float32 [1, 32], replicated, may hold values from 0.5 to 1.5
- norm_shift: float32 [1, 32], replicated, may hold values from -3 to 3
Outputs:
- activations: bfloat16 [2, 128, 128, 32, 128], P('col', 'gx', 'gy')
All inputs are finite; a program needn't handle non-finite values.
Results may differ from a plain program's by a relative error of at most 0.012.
Values may be sent and summed in bfloat16 or wider, within the bound.
A program may use at most 128 MiB of HBM per device.

v0:
```python
import math
import jax
import jax.numpy as jnp
from jax import lax
from jax.sharding import PartitionSpec as P

X = 128
Y = 128
Z = 128
MX = 16
MY = 16
MZ = 16
norm_eps = 1e-05


def signed_freqs(count):
    index = jnp.arange(count, dtype=jnp.int32)
    return jnp.where(index < count // 2, index, index - count)


def angles(positions, frequency, length):
    turn_count = positions[:, None] * frequency[None, :] % length
    return turn_count.astype(jnp.float32) * (2.0 * math.pi / length)


def forward_table(positions, frequency, length, factor):
    phase_angle = angles(positions, frequency, length)
    cosine = jnp.cos(phase_angle) * factor
    sine_part = jnp.sin(phase_angle) * factor
    from_real = jnp.stack([cosine, -sine_part], axis=-1)
    from_imag = jnp.stack([sine_part, cosine], axis=-1)
    return jnp.stack([from_real, from_imag], axis=1)


def inverse_table(frequency, positions, length):
    phase_angle = angles(positions, frequency, length).T
    cosine = jnp.cos(phase_angle)
    sine_part = jnp.sin(phase_angle)
    from_real = jnp.stack([cosine, sine_part], axis=-1)
    from_imag = jnp.stack([-sine_part, cosine], axis=-1)
    return jnp.stack([from_real, from_imag], axis=1)


def depth_tables(length, count):
    frequency = jnp.arange(count, dtype=jnp.int32)
    phase_angle = angles(jnp.arange(length, dtype=jnp.int32), frequency, length)
    forward = jnp.concatenate([jnp.cos(phase_angle), -jnp.sin(phase_angle)], axis=1)
    backward = jnp.concatenate([jnp.cos(phase_angle).T, -jnp.sin(phase_angle).T], axis=0)
    return (forward.astype(jnp.bfloat16), backward.astype(jnp.bfloat16))


def mix_modes(spectrum, weight):

    def contract(left, right):
        return jnp.einsum("abcz,abcdz->abdz", left, right, preferred_element_type=jnp.float32)

    real_in = spectrum[:, :, :, 0]
    imag_in = spectrum[:, :, :, 1]
    real_weight = weight[:, :, 0]
    imag_weight = weight[:, :, 1]
    real_out = contract(real_in, real_weight) - contract(imag_in, imag_weight)
    imag_out = contract(real_in, imag_weight) + contract(imag_in, real_weight)
    return jnp.stack([real_out, imag_out], axis=3)


def finish(spectral_part, skip_part, offset, scaling, shift_term):
    pre_norm = spectral_part + skip_part + offset[:, None]
    centre = jnp.mean(pre_norm, axis=2, keepdims=True)
    spread = jnp.mean(jnp.square(pre_norm - centre), axis=2, keepdims=True)
    normed = (pre_norm - centre) * lax.rsqrt(spread + norm_eps) * scaling[:, None] + shift_term[
        :, None
    ]
    return jax.nn.gelu(normed, approximate=False).astype(jnp.bfloat16)


def local(fields, spectral, skip_weight, skip_bias, norm_gain, norm_shift):
    highest = lax.Precision.HIGHEST
    hidden = fields[0]
    tile_first, tile_second, channels, depth_cells = hidden.shape
    first_cells = lax.axis_index("gx") * tile_first + jnp.arange(tile_first, dtype=jnp.int32)
    second_cells = lax.axis_index("gy") * tile_second + jnp.arange(tile_second, dtype=jnp.int32)
    depth_forward, depth_backward = depth_tables(Z, MZ)
    second_forward = forward_table(second_cells, signed_freqs(MY), Y, 1.0).astype(jnp.bfloat16)
    first_forward = forward_table(first_cells, signed_freqs(MX), X, 1.0 / math.sqrt(X * Y * Z))
    first_inverse = inverse_table(signed_freqs(MX), first_cells, X).astype(jnp.bfloat16)
    second_inverse = inverse_table(signed_freqs(MY), second_cells, Y)
    inverse_scale = 1.0 / math.sqrt(MX * MY * MZ)
    amplitude = jnp.dot(
        hidden.reshape(-1, depth_cells), depth_forward, preferred_element_type=jnp.float32
    )
    amplitude = amplitude.astype(jnp.bfloat16).reshape(tile_first, tile_second, channels, 2, MZ)
    along_second = jnp.einsum(
        "xycrz,yrks->xkcsz", amplitude, second_forward, preferred_element_type=jnp.float32
    )
    summed_second = lax.psum_scatter(
        along_second.astype(jnp.bfloat16), "gy", scatter_dimension=1, tiled=True
    ).astype(jnp.float32)
    partial_modes = jnp.einsum("xkcsz,xsjt->jkctz", summed_second, first_forward, precision=highest)
    summed = lax.psum_scatter(
        partial_modes.astype(jnp.bfloat16), "gx", scatter_dimension=0, tiled=True
    )
    weights_here = spectral[0]
    mixed_modes = mix_modes(summed, lax.all_gather(weights_here, "col", axis=4, tiled=True)).astype(
        jnp.bfloat16
    )
    gathered_second = lax.all_gather(mixed_modes, "gy", axis=1, tiled=True)
    full_modes = lax.all_gather(gathered_second, "gx", axis=0, tiled=True)
    rows_first = jnp.einsum(
        "jkcsz,jsxt->xkctz", full_modes, first_inverse, preferred_element_type=jnp.float32
    )
    rows_both = jnp.einsum(
        "xkcsz,ksyt->xyctz", rows_first, second_inverse, precision=highest
    ).astype(jnp.bfloat16)
    spectral_part = jnp.dot(
        rows_both.reshape(-1, 2 * MZ), depth_backward, preferred_element_type=jnp.float32
    )
    spectral_part = (
        spectral_part.reshape(tile_first, tile_second, channels, depth_cells) * inverse_scale
    )
    skip_part = jnp.einsum(
        "oc,xycz->xyoz", skip_weight[0], hidden, preferred_element_type=jnp.float32
    )
    hidden = finish(spectral_part, skip_part, skip_bias[0], norm_gain[0], norm_shift[0])
    return hidden[None]


def solution(mesh):
    placed = (
        P("col", "gx", "gy", None, None),
        P(None, "gx", "gy", None, None, "col", None),
        P(),
        P(),
        P(),
        P(),
    )
    return jax.shard_map(
        local,
        mesh=mesh,
        in_specs=placed,
        out_specs=P("col", "gx", "gy", None, None),
        check_vma=False,
    )
```

profile of v0, /device:TPU:0, one launch (start us, length us, event | category | flops | bytes accessed | tf_op | source)
XLA Modules:
  0.0 268.1 jit_solution(5952482807343169716)
XLA Ops:
  7.4 0.0 copy-start
  7.4 0.0 reduce-scatter.3.cloned.1.call-start
  7.4 0.1 negate_convert_fusion.1
  7.4 6.4 %fusion = bf16[32768,32]{0,1:T(8,128)(2,1)S(1)} fusion(bf16[32768,128]{1,0:T(8,128)(2,1)} %bitcast.159, bf16[128,16]{0,1:T(8,128)(2,1)S(1)} %get-tuple-element.37, bf16[128,16]{0,1:T(8,128)(2,1)S(1)} %get-tuple-element.38), kind=kOutput, calls=%fused_computation.1 | convolution fusion | flops 269500416 | bytes 10493952 | tf_op jit(solution)/shard_map/dot_general | solution.py:88
  13.8 7.9 %reshape.722 = bf16[32,32,32,2,16]{2,1,0,4,3:T(8,128)(2,1)} reshape(bf16[32768,32]{0,1:T(8,128)(2,1)S(1)} %fusion) | data formatting | bytes 4194304 | tf_op jit(solution)/shard_map/reshape | solution.py:91
  21.7 0.2 fusion.88
  21.9 4.7 %fusion.24 = bf16[32,16,32,2,16]{2,1,4,0,3:T(8,128)(2,1)S(1)} fusion(bf16[32,32,32,2,16]{2,1,0,4,3:T(8,128)(2,1)} %reshape.722, bf16[32,1,16,2]{0,2,1,3:T(8,128)(2,1)S(1)} %get-tuple-element.16, bf16[32,1,16,2]{0,2,1,3:T(8,128)(2,1)S(1)} %get-tuple-element.15), kind=kOutput, calls=%fused_computation.37 | convolution fusion | flops 67641344 | bytes 3149824 | tf_op jit(solution)/shard_map/xycrz,yrks->xkcsz/dot_general | solution.py:92
  26.6 3.1 %copy.26 = bf16[32,16,32,2,16]{2,4,3,0,1:T(8,128)(2,1)} copy(bf16[32,16,32,2,16]{2,1,4,0,3:T(8,128)(2,1)S(1)} %fusion.24) | data formatting | bytes 2097152 | tf_op jit(solution)/shard_map/convert_element_type | solution.py:96
  29.7 0.0 reduce-scatter.3.cloned.1.call-update
  29.7 0.0 all-gather.3.cloned.1.call-start
  29.8 0.5 all-gather.3.cloned.1.call-update
  30.3 0.2 reduce-scatter.5.cloned.1.call-start
  30.5 0.1 negate_convert_fusion
  30.6 0.2 fusion.85
  30.8 0.0 copy-done
  30.8 15.1 %fusion.13 = f32[32,32,128,32]{2,3,1,0:T(8,128)} fusion(bf16[1,32,32,32,128]{4,3,2,1,0:T(8,128)(2,1)} %param.6, bf16[1,32,32]{2,1,0:T(8,128)(2,1)S(1)} %copy-done), kind=kOutput, calls=%fused_computation.27 | convolution fusion | flops 268435456 | bytes 25167872 | tf_op jit(solution)/shard_map/oc,xycz->xyoz/dot_general | solution.py:120
  46.0 31.2 %reduce-scatter.3.cloned.1.call-done = bf16[32,4,32,2,16]{2,4,3,0,1:T(8,128)(2,1)} async-done(((bf16[32,16,32,2,16]{2,4,3,0,1:T(8,128)(2,1)}), bf16[32,4,32,2,16]{2,4,3,0,1:T(8,128)(2,1)}) %reduce-scatter.3.cloned.1.call-update) | async-done | bytes 262160 | tf_op jit(solution)/shard_map/reduce_scatter | solution.py:95
  77.2 1.9 fusion.30
  79.1 0.9 copy.29
  80.1 0.0 reduce-scatter.5.cloned.1.call-update
  80.1 11.0 %all-gather.3.cloned.1.call-done = bf16[1,4,4,2,32,32,16]{4,6,5,3,2,1,0:T(8,128)(2,1)} async-done(((bf16[1,4,4,2,32,16,16]{4,6,5,3,2,1,0:T(8,128)(2,1)}), bf16[1,4,4,2,32,32,16]{4,6,5,3,2,1,0:T(8,128)(2,1)}) %all-gather.3.cloned.1.call-update) | async-done | bytes 1048592 | tf_op jit(solution)/shard_map/all_gather | solution.py:103
  91.1 4.5 %slice_bitcast_fusion = (bf16[4,4,32,32,16]{2,4,3,1,0:T(8,128)(2,1)}, bf16[4,4,32,32,16]{2,4,3,1,0:T(8,128)(2,1)S(1)}) fusion(bf16[4,4,2,32,32,16]{3,5,4,2,1,0:T(8,128)(2,1)} %bitcast.161), kind=kLoop, calls=%fused_computation.39 | loop fusion | bytes 2097152 | tf_op jit(solution)/shard_map/squeeze | solution.py:60
  95.6 4.5 %copy.44 = bf16[4,4,32,32,16]{3,2,4,1,0:T(8,128)(2,1)} copy(bf16[4,4,32,32,16]{2,4,3,1,0:T(8,128)(2,1)} %get-tuple-element.5) | data formatting | bytes 1048576 | tf_op jit(solution)/shard_map/squeeze | solution.py:60
  100.2 2.9 %copy.41 = bf16[4,4,32,32,16]{3,2,4,1,0:T(8,128)(2,1)} copy(bf16[4,4,32,32,16]{2,4,3,1,0:T(8,128)(2,1)S(1)} %get-tuple-element.6) | data formatting | bytes 1048576 | tf_op jit(solution)/shard_map/squeeze | solution.py:59
  103.1 0.0 reduce-scatter.5.cloned.1.call-done
  103.1 0.9 slice_bitcast_fusion.3
  104.0 2.2 fusion.39
  106.2 2.3 fusion.37
  108.5 2.3 fusion.35
  110.7 2.2 fusion.41
  113.1 7.2 %all_gather.10 = bf16[4,16,32,2,16]{2,4,3,0,1:T(8,128)(2,1)S(1)} all-gather(bf16[4,4,32,2,16]{2,4,3,0,1:T(8,128)(2,1)S(1)} %pad_maximum_fusion), channel_id=1, replica_groups=mesh['gx'=4,'gy'=4,'col'=2] {'gy'}, dimensions={1}, use_global_device_ids=true | all-gather | bytes 163840 | tf_op jit(solution)/shard_map/all_gather | solution.py:106
  120.3 38.6 %all_gather.11 = bf16[16,16,32,2,16]{2,4,3,1,0:T(8,128)(2,1)S(1)} all-gather(bf16[4,16,32,2,16]{2,4,3,1,0:T(8,128)(2,1)S(1)} %copy.30), channel_id=1, replica_groups=mesh['gx'=4,'gy'=4,'col'=2] {'gx'}, dimensions={0}, use_global_device_ids=true | all-gather | bytes 655360 | tf_op jit(solution)/shard_map/all_gather | solution.py:107
  158.8 1.5 convolution_bitcast_fusion
  160.3 0.0 copy-start.4
  160.3 22.8 %fusion.12 = bf16[32,32,32,2,16]{2,1,4,0,3:T(8,128)(2,1)} fusion(f32[32,16,32,2,16]{2,0,4,1,3:T(8,128)S(1)} %convolution_bitcast_fusion, f32[16,1,32,2]{2,0,3,1:T(8,128)S(1)} %get-tuple-element.10, f32[16,1,32,2]{2,0,3,1:T(8,128)S(1)} %get-tuple-element.9), kind=kOutput, calls=%fused_computation.26 | convolution fusion | flops 403703808 | bytes 4202496 | tf_op jit(solution)/shard_map/xkcsz,ksyt->xyctz/dot_general | solution.py:111
  183.1 10.5 %copy.34 = bf16[32,32,32,2,16]{2,4,3,1,0:T(8,128)(2,1)} copy(bf16[32,32,32,2,16]{2,1,4,0,3:T(8,128)(2,1)} %fusion.12) | data formatting | bytes 4194304 | tf_op jit(solution)/shard_map/convert_element_type | solution.py:113
  193.6 0.0 copy-done.4
  193.6 14.5 %fusion.93 = (f32[32,32,128]{2,1,0:T(8,128)S(1)}, f32[32,32,32,128]{3,2,1,0:T(8,128)}) fusion(f32[32]{0:T(128)S(1)} %bitcast.164, f32[32,32,128,32]{2,3,1,0:T(8,128)} %fusion.13, bf16[32,32,32,32]{2,3,1,0:T(8,128)(2,1)} %bitcast.160, bf16[16,128]{1,0:T(8,128)(2,1)S(1)} %get-tuple-element.41, bf16[16,128]{1,0:T(8,128)(2,1)S(1)} %get-tuple-element.42), kind=kOutput, calls=%fused_computation.167 | convolution fusion | flops 285097984 | bytes 36184192 | tf_op jit(solution)/shard_map/dot_general | solution.py:114
  208.1 0.0 copy-start.2
  208.1 0.0 copy-start.3
  208.2 0.0 copy-start.1
  208.2 10.9 %multiply_reduce_fusion = f32[32,32,128]{2,1,0:T(8,128)S(1)} fusion(f32[32,32,32,128]{3,2,1,0:T(8,128)} %get-tuple-element.36, f32[32,32,128]{2,1,0:T(8,128)S(1)} %broadcast_multiply_fusion), kind=kLoop, calls=%fused_computation.23 | loop fusion | flops 12451840 | bytes 17825792 | tf_op jit(solution)/shard_map/reduce_sum | solution.py:69
  219.1 0.1 add_rsqrt_fusion
  219.2 0.0 copy-done.2
  219.2 0.0 copy-done.3
  219.2 41.4 %fusion.21 = bf16[1,32,32,32,128]{4,3,2,1,0:T(8,128)(2,1)} fusion(f32[32]{0:T(128)S(1)} %bitcast.162, f32[32]{0:T(128)S(1)} %bitcast.163, f32[32,32,128]{2,1,0:T(8,128)S(1)} %add_rsqrt_fusion, f32[32,32,32,128]{3,2,1,0:T(8,128)} %get-tuple-element.36, f32[32,32,128]{2,1,0:T(8,128)S(1)} %broadcast_multiply_fusion), kind=kLoop, calls=%fused_computation.36 | loop fusion | flops 289406976 | bytes 26214656 | tf_op jit(solution)/shard_map/broadcast_in_dim | solution.py:124
  260.6 0.0 copy-done.1
  (11 shorter events, 0.2 us)
Async XLA Ops:
  7.4 23.4 %copy-start = (bf16[1,32,32]{2,1,0:T(8,128)(2,1)S(1)}, bf16[1,32,32]{2,1,0:T(8,128)(2,1)}, u32[]{:S(2)}) copy-start(bf16[1,32,32]{2,1,0:T(8,128)(2,1)} %param.8) | copy-start | bytes 6148
  7.4 69.8 %reduce-scatter.3.cloned.1.call-start = ((), (), s32[]{:S(2)}) async-start(), calls=%async_computation.2 | async-start | bytes 5242880 | tf_op jit(solution)/shard_map/reduce_scatter | solution.py:95
  29.7 61.4 %all-gather.3.cloned.1.call-start = ((), (), s32[]{:S(2)}) async-start(), calls=%async_computation.4 | async-start | bytes 6291456 | tf_op jit(solution)/shard_map/all_gather | solution.py:103
  30.3 72.8 %reduce-scatter.5.cloned.1.call-start = ((), (), s32[]{:S(2)}) async-start(), calls=%async_computation.3 | async-start | bytes 655360 | tf_op jit(solution)/shard_map/reduce_scatter | solution.py:99
  160.3 33.3 %copy-start.4 = (f32[1,32]{1,0:T(1,128)S(1)}, f32[1,32]{1,0:T(1,128)}, u32[]{:S(2)}) copy-start(f32[1,32]{1,0:T(1,128)} %param.9) | copy-start | bytes 388
  208.1 11.1 %copy-start.2 = (f32[1,32]{1,0:T(1,128)S(1)}, f32[1,32]{1,0:T(1,128)}, u32[]{:S(2)}) copy-start(f32[1,32]{1,0:T(1,128)} %param.11) | copy-start | bytes 388
  208.1 11.1 %copy-start.3 = (f32[1,32]{1,0:T(1,128)S(1)}, f32[1,32]{1,0:T(1,128)}, u32[]{:S(2)}) copy-start(f32[1,32]{1,0:T(1,128)} %param.10) | copy-start | bytes 388
  208.2 52.5 %copy-start.1 = (bf16[1,32,32]{2,1,0:T(8,128)(2,1)S(1)}, bf16[1,32,32]{2,1,0:T(8,128)(2,1)}, u32[]{:S(2)}) copy-start(bf16[1,32,32]{2,1,0:T(8,128)(2,1)} %param.8) | copy-start | bytes 6148
Sparse Core Ops, SparseCore 0:
  29.9 47.2 reduce-scatter.2
  80.2 21.8 reduce-scatter.4
Sparse Core Ops, SparseCore 1:
  31.8 59.3 all-gather.2
where the time goes:
time: 269 us; the launch traced here: 268 us
  matrix products  75.9 us (28%)
  other arithmetic  53 us (20%)
  blocking collectives  45.7 us (17%)
  waiting for transfers between devices  42.8 us (16%)
  local copies, waits for them, and re-layouts  35.4 us (13%)
  between operations  15 us (6%)
    broadcast_in_dim x1, other arithmetic, local(): return hidden[None]  41.4 us
    all_gather x1, blocking collectives, local(): full_modes = lax.all_gather(gathered_second, 'gx', axis=0, tiled=True)  38.6 us
    reduce_scatter x1, waiting for transfers between devices, local(): lax.psum_scatter(along_second.astype(jnp.bfloat16), 'gy', scatter_dimensi...  31.2 us
    dot_general x1, matrix products, local(): jnp.einsum('xkcsz,ksyt->xyctz', rows_first, second_inverse, precision=hig...  22.8 us
    dot_general x1, matrix products, local(): jnp.einsum('oc,xycz->xyoz', skip_weight[0], hidden, preferred_element_typ...  15.1 us
    dot_general x1, matrix products, local(): jnp.dot(rows_both.reshape(-1, 2 * MZ), depth_backward, preferred_element_...  14.5 us
    all_gather x1, waiting for transfers between devices, local(): lax.all_gather(weights_here, 'col', axis=4, tiled=True)  11 us
    reduce_sum x1, other arithmetic, finish(): spread = jnp.mean(jnp.square(pre_norm - centre), axis=2, keepdims=True)  10.9 us
  transfers between devices with their start and end apart: 3, of which 2 were waited for; matrix products, arithmetic and copies ran while one was open for 11% of the time, Pallas kernels for 0%

commit v1 on v0

--- a/solution.py
+++ b/solution.py
@@ -74,6 +74,22 @@
 
 
 def local(fields, spectral, skip_weight, skip_bias, norm_gain, norm_shift):
+
+    def _list_sides(vector, inner_x):
+        new = jax.lax.axis_index("gx")
+        b_now = jax.lax.axis_size("gx")
+        high, y_new, then = (b_now, new, vector.shape[0])
+        t1 = range(high)
+        extra = map(lambda w: (w, (w + 1) % high), t1)
+        blocks_here = list(extra)
+        current_arr, heard = (vector, None)
+        for kk in range(high):
+            back = jax.lax.ppermute(current_arr, "gx", blocks_here) if kk < high - 1 else None
+            inter = inner_x(current_arr, (y_new - kk) % high * then)
+            heard = inter if heard is None else heard + inter
+            current_arr = back
+        return heard
+
     highest = lax.Precision.HIGHEST
     hidden = fields[0]
     tile_first, tile_second, channels, depth_cells = hidden.shape
@@ -104,9 +120,14 @@
         jnp.bfloat16
     )
     gathered_second = lax.all_gather(mixed_modes, "gy", axis=1, tiled=True)
-    full_modes = lax.all_gather(gathered_second, "gx", axis=0, tiled=True)
-    rows_first = jnp.einsum(
-        "jkcsz,jsxt->xkctz", full_modes, first_inverse, preferred_element_type=jnp.float32
+    rows_first = _list_sides(
+        gathered_second,
+        lambda part, offset_2: jnp.einsum(
+            "jkcsz,jsxt->xkctz",
+            part,
+            lax.dynamic_slice_in_dim(first_inverse, offset_2, part.shape[0], axis=0),
+            preferred_element_type=jnp.float32,
+        ),
     )
     rows_both = jnp.einsum(
         "xkcsz,ksyt->xyctz", rows_first, second_inverse, precision=highest

time: 269 us -> 287 us (1.067); the launches traced: 268 us -> 282 us
  blocking collectives: 45.7 us -> 7.15 us
  waiting for transfers between devices: 42.8 us -> 75.1 us
  matrix products: 75.9 us -> 93.1 us
    all_gather x1 -> x0, blocking collectives: 38.6 us -> none  [local(): full_modes = lax.all_gather(gathered_second, 'gx', axis=0, tiled=True)]
    ppermute x0 -> x3, waiting for transfers between devices: none -> 32.8 us  [_list_sides(): jax.lax.ppermute(current_arr, 'gx', blocks_here)]
    dot_general x1 -> x4, matrix products: 1.49 us -> 18.6 us  [local(): jnp.einsum('jkcsz,jsxt->xkctz', part, lax.dynamic_slice_in_dim(first_inve...]
  transfers between devices with their start and end apart: 3 -> 6, of which waited for: 2 -> 5; matrix products, arithmetic and copies ran while one was open for 11% -> 15% of each run, Pallas kernels for 0% -> 0%
where the time goes in v1:
time: 287 us; the launch traced here: 282 us
  matrix products  93.1 us (32%)
  waiting for transfers between devices  75.1 us (26%)
  other arithmetic  53 us (18%)
  local copies, waits for them, and re-layouts  35.7 us (12%)
  between operations  15.4 us (5%)
  blocking collectives  7.15 us (2%)
    broadcast_in_dim x1, other arithmetic, local(): return hidden[None]  41.4 us
    ppermute x3, waiting for transfers between devices, _list_sides(): jax.lax.ppermute(current_arr, 'gx', blocks_here)  32.8 us
    reduce_scatter x1, waiting for transfers between devices, local(): lax.psum_scatter(along_second.astype(jnp.bfloat16), 'gy', scatter_dimensi...  30.7 us
    dot_general x1, matrix products, local(): jnp.einsum('xkcsz,ksyt->xyctz', rows_first, second_inverse, precision=hig...  22.8 us
    dot_general x4, matrix products, local(): jnp.einsum('jkcsz,jsxt->xkctz', part, lax.dynamic_slice_in_dim(first_inve...  18.6 us
    dot_general x1, matrix products, local(): jnp.einsum('oc,xycz->xyoz', skip_weight[0], hidden, preferred_element_typ...  15.2 us
    dot_general x1, matrix products, local(): jnp.dot(rows_both.reshape(-1, 2 * MZ), depth_backward, preferred_element_...  14.4 us
    all_gather x1, waiting for transfers between devices, local(): lax.all_gather(weights_here, 'col', axis=4, tiled=True)  11 us
  transfers between devices with their start and end apart: 6, of which 5 were waited for; matrix products, arithmetic and copies ran while one was open for 15% of the time, Pallas kernels for 0%

profile of v1, /device:TPU:0, one launch (start us, length us, event | category | flops | bytes accessed | tf_op | source)
XLA Modules:
  0.0 281.6 jit_solution(13112532591744908951)
XLA Ops:
  7.4 0.0 copy-start
  7.4 0.0 reduce-scatter.3.cloned.1.call-start
  7.4 0.1 negate_convert_fusion.1
  7.4 6.4 %fusion = bf16[32768,32]{0,1:T(8,128)(2,1)S(1)} fusion(bf16[32768,128]{1,0:T(8,128)(2,1)} %bitcast.198, bf16[128,16]{0,1:T(8,128)(2,1)S(1)} %get-tuple-element.37, bf16[128,16]{0,1:T(8,128)(2,1)S(1)} %get-tuple-element.38), kind=kOutput, calls=%fused_computation.1 | convolution fusion | flops 269500416 | bytes 10493952 | tf_op jit(solution)/shard_map/dot_general | solution.py:104
  13.8 7.9 %reshape.722 = bf16[32,32,32,2,16]{2,1,0,4,3:T(8,128)(2,1)} reshape(bf16[32768,32]{0,1:T(8,128)(2,1)S(1)} %fusion) | data formatting | bytes 4194304 | tf_op jit(solution)/shard_map/reshape | solution.py:107
  21.7 0.2 fusion.104
  21.9 4.7 %fusion.25 = bf16[32,16,32,2,16]{2,1,4,0,3:T(8,128)(2,1)S(1)} fusion(bf16[32,32,32,2,16]{2,1,0,4,3:T(8,128)(2,1)} %reshape.722, bf16[32,1,16,2]{0,2,1,3:T(8,128)(2,1)S(1)} %get-tuple-element.16, bf16[32,1,16,2]{0,2,1,3:T(8,128)(2,1)S(1)} %get-tuple-element.15), kind=kOutput, calls=%fused_computation.41 | convolution fusion | flops 67641344 | bytes 3149824 | tf_op jit(solution)/shard_map/xycrz,yrks->xkcsz/dot_general | solution.py:108
  26.6 3.1 %copy.26 = bf16[32,16,32,2,16]{2,4,3,0,1:T(8,128)(2,1)} copy(bf16[32,16,32,2,16]{2,1,4,0,3:T(8,128)(2,1)S(1)} %fusion.25) | data formatting | bytes 2097152 | tf_op jit(solution)/shard_map/convert_element_type | solution.py:112
  29.7 0.0 reduce-scatter.3.cloned.1.call-update
  29.7 0.0 all-gather.3.cloned.1.call-start
  29.8 0.5 all-gather.3.cloned.1.call-update
  30.3 0.5 reduce-scatter.5.cloned.1.call-start
  30.8 0.2 fusion.101
  31.1 0.1 negate_convert_fusion
  31.2 0.0 copy-done
  31.2 15.2 %fusion.13 = f32[32,32,128,32]{2,3,1,0:T(8,128)} fusion(bf16[1,32,32,32,128]{4,3,2,1,0:T(8,128)(2,1)} %param.6, bf16[1,32,32]{2,1,0:T(8,128)(2,1)S(1)} %copy-done), kind=kOutput, calls=%fused_computation.27 | convolution fusion | flops 268435456 | bytes 25167872 | tf_op jit(solution)/shard_map/oc,xycz->xyoz/dot_general | solution.py:141
  46.5 30.7 %reduce-scatter.3.cloned.1.call-done = bf16[32,4,32,2,16]{2,4,3,0,1:T(8,128)(2,1)} async-done(((bf16[32,16,32,2,16]{2,4,3,0,1:T(8,128)(2,1)}), bf16[32,4,32,2,16]{2,4,3,0,1:T(8,128)(2,1)}) %reduce-scatter.3.cloned.1.call-update) | async-done | bytes 262160 | tf_op jit(solution)/shard_map/reduce_scatter | solution.py:111
  77.2 1.9 fusion.29
  79.1 0.9 copy.29
  80.1 0.0 reduce-scatter.5.cloned.1.call-update
  80.1 11.0 %all-gather.3.cloned.1.call-done = bf16[1,4,4,2,32,32,16]{4,6,5,3,2,1,0:T(8,128)(2,1)} async-done(((bf16[1,4,4,2,32,16,16]{4,6,5,3,2,1,0:T(8,128)(2,1)}), bf16[1,4,4,2,32,32,16]{4,6,5,3,2,1,0:T(8,128)(2,1)}) %all-gather.3.cloned.1.call-update) | async-done | bytes 1048592 | tf_op jit(solution)/shard_map/all_gather | solution.py:119
  91.1 4.5 %slice_bitcast_fusion = (bf16[4,4,32,32,16]{2,4,3,1,0:T(8,128)(2,1)}, bf16[4,4,32,32,16]{2,4,3,1,0:T(8,128)(2,1)S(1)}) fusion(bf16[4,4,2,32,32,16]{3,5,4,2,1,0:T(8,128)(2,1)} %bitcast.200), kind=kLoop, calls=%fused_computation.42 | loop fusion | bytes 2097152 | tf_op jit(solution)/shard_map/squeeze | solution.py:60
  95.6 4.5 %copy.44 = bf16[4,4,32,32,16]{3,2,4,1,0:T(8,128)(2,1)} copy(bf16[4,4,32,32,16]{2,4,3,1,0:T(8,128)(2,1)} %get-tuple-element.5) | data formatting | bytes 1048576 | tf_op jit(solution)/shard_map/squeeze | solution.py:60
  100.2 2.9 %copy.41 = bf16[4,4,32,32,16]{3,2,4,1,0:T(8,128)(2,1)} copy(bf16[4,4,32,32,16]{2,4,3,1,0:T(8,128)(2,1)S(1)} %get-tuple-element.6) | data formatting | bytes 1048576 | tf_op jit(solution)/shard_map/squeeze | solution.py:59
  103.1 0.0 reduce-scatter.5.cloned.1.call-done
  103.1 0.9 slice_bitcast_fusion.3
  104.0 2.2 fusion.43
  106.2 2.2 fusion.41
  108.5 2.3 fusion.47
  110.7 2.3 fusion.45
  113.1 7.2 %all_gather.7 = bf16[4,16,32,2,16]{2,4,3,0,1:T(8,128)(2,1)S(1)} all-gather(bf16[4,4,32,2,16]{2,4,3,0,1:T(8,128)(2,1)S(1)} %pad_maximum_fusion), channel_id=1, replica_groups=mesh['gx'=4,'gy'=4,'col'=2] {'gy'}, dimensions={1}, use_global_device_ids=true | all-gather | bytes 163840 | tf_op jit(solution)/shard_map/all_gather | solution.py:122
  120.2 0.3 copy.30
  120.5 1.5 collective-permute-start
  122.0 1.5 fusion.37
  123.5 13.0 %collective-permute-done = bf16[4,16,32,2,16]{2,0,3,4,1:T(4,128)(2,1)S(1)} collective-permute-done((bf16[4,16,32,2,16]{2,0,3,4,1:T(4,128)(2,1)S(1)}, bf16[4,16,32,2,16]{2,0,3,4,1:T(4,128)(2,1)S(1)}, u32[]{:S(2)}, u32[]{:S(2)}) %collective-permute-start) | collective-permute-done | bytes 131104 | tf_op jit(solution)/shard_map/ppermute | solution.py:87
  136.5 0.0 collective-permute-start.1
  136.5 4.7 %fusion.35 = f32[32,2,16,32,16,1]{3,0,5,4,2,1:T(8,128)} fusion(bf16[4,16,32,2,16]{2,0,3,4,1:T(4,128)(2,1)S(1)} %collective-permute-done, s32[]{:T(128)S(6)} %select_n.151, bf16[16,1,32,2]{2,0,1,3:T(8,128)(2,1)S(1)} %get-tuple-element.14, bf16[16,1,32,2]{2,0,1,3:T(8,128)(2,1)S(1)} %get-tuple-element.13), kind=kOutput, calls=%fused_computation.52 | convolution fusion | flops 8390656 | bytes 2232324 | tf_op jit(solution)/shard_map/jkcsz,jsxt->xkctz/dot_general | solution.py:125
  141.3 10.4 %collective-permute-done.1 = bf16[4,16,32,2,16]{2,0,3,4,1:T(4,128)(2,1)S(1)} collective-permute-done((bf16[4,16,32,2,16]{2,0,3,4,1:T(4,128)(2,1)S(1)}, bf16[4,16,32,2,16]{2,0,3,4,1:T(4,128)(2,1)S(1)}, u32[]{:S(2)}, u32[]{:S(2)}) %collective-permute-start.1) | collective-permute-done | bytes 131104 | tf_op jit(solution)/shard_map/ppermute | solution.py:87
  151.7 0.2 collective-permute-start.2
  151.8 4.9 %fusion.33 = f32[32,2,16,32,16,1]{3,0,5,4,2,1:T(8,128)} fusion(bf16[4,16,32,2,16]{2,0,3,4,1:T(4,128)(2,1)S(1)} %collective-permute-done.1, s32[]{:T(128)S(6)} %select_n.153, bf16[16,1,32,2]{2,0,1,3:T(8,128)(2,1)S(1)} %get-tuple-element.14, bf16[16,1,32,2]{2,0,1,3:T(8,128)(2,1)S(1)} %get-tuple-element.13), kind=kOutput, calls=%fused_computation.50 | convolution fusion | flops 8390656 | bytes 2232324 | tf_op jit(solution)/shard_map/jkcsz,jsxt->xkctz/dot_general | solution.py:125
  156.7 9.4 %collective-permute-done.2 = bf16[4,16,32,2,16]{2,0,3,4,1:T(4,128)(2,1)S(1)} collective-permute-done((bf16[4,16,32,2,16]{2,0,3,4,1:T(4,128)(2,1)S(1)}, bf16[4,16,32,2,16]{2,0,3,4,1:T(4,128)(2,1)S(1)}, u32[]{:S(2)}, u32[]{:S(2)}) %collective-permute-start.2) | collective-permute-done | bytes 131104 | tf_op jit(solution)/shard_map/ppermute | solution.py:87
  166.1 7.6 %fusion.17 = f32[32,16,32,2,16]{2,0,4,1,3:T(8,128)S(1)} fusion(f32[32,2,16,32,16,1]{3,0,5,4,2,1:T(8,128)} %fusion.33, f32[32,2,16,32,16,1]{3,0,5,4,2,1:T(8,128)} %fusion.35, f32[32,2,16,32,16,1]{3,0,5,4,2,1:T(8,128)S(1)} %fusion.37, bf16[4,16,32,2,16]{2,0,3,4,1:T(4,128)(2,1)S(1)} %collective-permute-done.2, s32[]{:T(128)S(6)} %select_n.155, ...), kind=kOutput, calls=%fused_computation.32 | convolution fusion | flops 9963520 | bytes 8523780 | tf_op jit(solution)/shard_map/jkcsz,jsxt->xkctz/dot_general | solution.py:125
  173.6 0.0 copy-start.4
  173.7 22.8 %fusion.12 = bf16[32,32,32,2,16]{2,1,4,0,3:T(8,128)(2,1)} fusion(f32[32,16,32,2,16]{2,0,4,1,3:T(8,128)S(1)} %fusion.17, f32[16,1,32,2]{2,0,3,1:T(8,128)S(1)} %get-tuple-element.10, f32[16,1,32,2]{2,0,3,1:T(8,128)S(1)} %get-tuple-element.9), kind=kOutput, calls=%fused_computation.26 | convolution fusion | flops 403703808 | bytes 4202496 | tf_op jit(solution)/shard_map/xkcsz,ksyt->xyctz/dot_general | solution.py:132
  196.4 10.5 %copy.34 = bf16[32,32,32,2,16]{2,4,3,1,0:T(8,128)(2,1)} copy(bf16[32,32,32,2,16]{2,1,4,0,3:T(8,128)(2,1)} %fusion.12) | data formatting | bytes 4194304 | tf_op jit(solution)/shard_map/convert_element_type | solution.py:134
  207.0 0.0 copy-done.4
  207.0 14.4 %fusion.117 = (f32[32,32,128]{2,1,0:T(8,128)S(1)}, f32[32,32,32,128]{3,2,1,0:T(8,128)}) fusion(f32[32]{0:T(128)S(1)} %bitcast.203, f32[32,32,128,32]{2,3,1,0:T(8,128)} %fusion.13, bf16[32,32,32,32]{2,3,1,0:T(8,128)(2,1)} %bitcast.199, bf16[16,128]{1,0:T(8,128)(2,1)S(1)} %get-tuple-element.41, bf16[16,128]{1,0:T(8,128)(2,1)S(1)} %get-tuple-element.42), kind=kOutput, calls=%fused_computation.196 | convolution fusion | flops 285097984 | bytes 36184192 | tf_op jit(solution)/shard_map/dot_general | solution.py:135
  221.4 0.0 copy-start.2
  221.4 0.0 copy-start.3
  221.4 0.0 copy-start.1
  221.5 10.9 %multiply_reduce_fusion = f32[32,32,128]{2,1,0:T(8,128)S(1)} fusion(f32[32,32,32,128]{3,2,1,0:T(8,128)} %get-tuple-element.36, f32[32,32,128]{2,1,0:T(8,128)S(1)} %broadcast_multiply_fusion), kind=kLoop, calls=%fused_computation.23 | loop fusion | flops 12451840 | bytes 17825792 | tf_op jit(solution)/shard_map/reduce_sum | solution.py:69
  232.4 0.1 add_rsqrt_fusion
  232.5 0.0 copy-done.2
  232.5 0.0 copy-done.3
  232.5 41.4 %fusion.22 = bf16[1,32,32,32,128]{4,3,2,1,0:T(8,128)(2,1)} fusion(f32[32]{0:T(128)S(1)} %bitcast.201, f32[32]{0:T(128)S(1)} %bitcast.202, f32[32,32,128]{2,1,0:T(8,128)S(1)} %add_rsqrt_fusion, f32[32,32,32,128]{3,2,1,0:T(8,128)} %get-tuple-element.36, f32[32,32,128]{2,1,0:T(8,128)S(1)} %broadcast_multiply_fusion), kind=kLoop, calls=%fused_computation.40 | loop fusion | flops 289406976 | bytes 26214656 | tf_op jit(solution)/shard_map/broadcast_in_dim | solution.py:145
  273.9 0.0 copy-done.1
  (10 shorter events, 0.2 us)
Async XLA Ops:
  7.4 23.8 %copy-start = (bf16[1,32,32]{2,1,0:T(8,128)(2,1)S(1)}, bf16[1,32,32]{2,1,0:T(8,128)(2,1)}, u32[]{:S(2)}) copy-start(bf16[1,32,32]{2,1,0:T(8,128)(2,1)} %param.8) | copy-start | bytes 6148
  7.4 69.8 %reduce-scatter.3.cloned.1.call-start = ((), (), s32[]{:S(2)}) async-start(), calls=%async_computation.2 | async-start | bytes 5242880 | tf_op jit(solution)/shard_map/reduce_scatter | solution.py:111
  29.7 61.4 %all-gather.3.cloned.1.call-start = ((), (), s32[]{:S(2)}) async-start(), calls=%async_computation.4 | async-start | bytes 6291456 | tf_op jit(solution)/shard_map/all_gather | solution.py:119
  30.3 72.8 %reduce-scatter.5.cloned.1.call-start = ((), (), s32[]{:S(2)}) async-start(), calls=%async_computation.3 | async-start | bytes 655360 | tf_op jit(solution)/shard_map/reduce_scatter | solution.py:115
  120.5 16.0 %collective-permute-start = (bf16[4,16,32,2,16]{2,0,3,4,1:T(4,128)(2,1)S(1)}, bf16[4,16,32,2,16]{2,0,3,4,1:T(4,128)(2,1)S(1)}, u32[]{:S(2)}, u32[]{:S(2)}) collective-permute-start(bf16[4,16,32,2,16]{2,0,3,4,1:T(4,128)(2,1)S(1)} %copy.30), channel_id=1, source_target_pairs={{0,8},{8,16},{16,24},{24,0},{1,9},{9,17},{17,25},{25,1},{2,10},{10... | collective-permute-start | bytes 393224 | tf_op jit(solution)/shard_map/ppermute | solution.py:87
  136.5 15.1 %collective-permute-start.1 = (bf16[4,16,32,2,16]{2,0,3,4,1:T(4,128)(2,1)S(1)}, bf16[4,16,32,2,16]{2,0,3,4,1:T(4,128)(2,1)S(1)}, u32[]{:S(2)}, u32[]{:S(2)}) collective-permute-start(bf16[4,16,32,2,16]{2,0,3,4,1:T(4,128)(2,1)S(1)} %collective-permute-done), channel_id=1, source_target_pairs={{0,8},{8,16},{16,24},{24,0},{1,9},{9,17},{17,25},{25,1},{2,10},{10... | collective-permute-start | bytes 393224 | tf_op jit(solution)/shard_map/ppermute | solution.py:87
  151.7 14.4 %collective-permute-start.2 = (bf16[4,16,32,2,16]{2,0,3,4,1:T(4,128)(2,1)S(1)}, bf16[4,16,32,2,16]{2,0,3,4,1:T(4,128)(2,1)S(1)}, u32[]{:S(2)}, u32[]{:S(2)}) collective-permute-start(bf16[4,16,32,2,16]{2,0,3,4,1:T(4,128)(2,1)S(1)} %collective-permute-done.1), channel_id=1, source_target_pairs={{0,8},{8,16},{16,24},{24,0},{1,9},{9,17},{17,25},{25,1},{2,10},{10... | collective-permute-start | bytes 393224 | tf_op jit(solution)/shard_map/ppermute | solution.py:87
  173.6 33.3 %copy-start.4 = (f32[1,32]{1,0:T(1,128)S(1)}, f32[1,32]{1,0:T(1,128)}, u32[]{:S(2)}) copy-start(f32[1,32]{1,0:T(1,128)} %param.9) | copy-start | bytes 388
  221.4 11.1 %copy-start.2 = (f32[1,32]{1,0:T(1,128)S(1)}, f32[1,32]{1,0:T(1,128)}, u32[]{:S(2)}) copy-start(f32[1,32]{1,0:T(1,128)} %param.11) | copy-start | bytes 388
  221.4 11.1 %copy-start.3 = (f32[1,32]{1,0:T(1,128)S(1)}, f32[1,32]{1,0:T(1,128)}, u32[]{:S(2)}) copy-start(f32[1,32]{1,0:T(1,128)} %param.10) | copy-start | bytes 388
  221.4 52.5 %copy-start.1 = (bf16[1,32,32]{2,1,0:T(8,128)(2,1)S(1)}, bf16[1,32,32]{2,1,0:T(8,128)(2,1)}, u32[]{:S(2)}) copy-start(bf16[1,32,32]{2,1,0:T(8,128)(2,1)} %param.8) | copy-start | bytes 6148
Sparse Core Ops, SparseCore 0:
  29.9 47.2 reduce-scatter.2
  80.2 21.8 reduce-scatter.4
Sparse Core Ops, SparseCore 1:
  31.8 59.3 all-gather.2
